TPU v7x, 32 devices: a whole 2x2x4 slice. The times are simulated.
32 devices in a mesh: sec: 2 (over y), ty: 16 (over z, x, core).
Axes of the slice: x: 2, y: 2, z: 4, core: 2. Of those that a mesh axis runs over, the one named last changes fastest.
Arguments:
- points: float32 [4, 32768], P(None, ('sec', 'ty')), parts along dimension 1, may hold values from -88 to 2136, as said below
- source: bfloat16 [1024, 2048], P(('sec', 'ty')), parts along dimension 0, may hold values from -4 to 4
- slab_first: int32 [32], P(('sec', 'ty')), parts along dimension 0, may hold values from 0 to 29, as said below
- slab_count: int32 [32], P(('sec', 'ty')), parts along dimension 0, may hold values from 3 to 6, as said below
Outputs:
- rendered: bfloat16 [1024, 2048], P(('sec', 'ty')), parts along dimension 0
- vertex_affines: float32 [6, 128, 256], P(None, ('sec', 'ty')), parts along dimension 1
There are 2 independent parts, one for each index of `sec`. A program takes and returns all parts, laid end to end along the dimension named above; each array names one. Nothing has to cross between parts.
Inputs may be any that keep to these rules, and one draw needn't show every extreme that they name: `points`: for tile t, rows 0 and 1 are fixed positions: each 16 x 16 pixel cell of rows t*32 to (t+1)*32 and columns 0 to 2048 holds 4 of them, listed cell by cell, cells in row-major order; rows 2 and 3 are the matching moving positions. Source block j is rows j*16 to (j+1)*16 - 1. Tile t samples blocks slab_first[t] to slab_first[t] + slab_count[t] - 1, all within rows (t-1)*32 to (t+2)*32 - 1. slab_count reaches 6 on some tile in every draw.
All inputs are finite; a program needn't handle non-finite values.
Results may differ from a plain program's by a relative error of at most 0.008.
Values may be sent and summed in bfloat16 or wider, within the bound.
A program may use at most 64 MiB of HBM per device.

v0:
```python
import math

import jax
import jax.numpy as jnp
from jax import lax
from jax.experimental import pallas as pl
from jax.experimental.pallas import tpu as pltpu
from jax.sharding import PartitionSpec as P

W = 2048
BH = 16
SP = 8
H = 32
K = 6
VR = 4
VC = 256


MESH = pl.DeviceIdType.MESH
RIDGE_TERM = 0.01


def solve_affine(moments, vertex_x, vertex_y):
    scale = 1.0 / moments[0]
    mean_px, mean_py, mean_qx, mean_qy = [m * scale for m in moments[1:5]]
    cov_xx = moments[5] * scale - mean_px * mean_px + RIDGE_TERM
    cov_xy = moments[6] * scale - mean_px * mean_py
    cov_yy = moments[7] * scale - mean_py * mean_py + RIDGE_TERM
    cross_xx = moments[8] * scale - mean_qx * mean_px
    cross_xy = moments[9] * scale - mean_qx * mean_py
    cross_yx = moments[10] * scale - mean_qy * mean_px
    cross_yy = moments[11] * scale - mean_qy * mean_py
    inverse = 1.0 / (cov_xx * cov_yy - cov_xy * cov_xy)
    lin_xx = (cross_xx * cov_yy - cross_xy * cov_xy) * inverse
    lin_xy = (cross_xy * cov_xx - cross_xx * cov_xy) * inverse
    lin_yx = (cross_yx * cov_yy - cross_yy * cov_xy) * inverse
    lin_yy = (cross_yy * cov_xx - cross_yx * cov_xy) * inverse
    delta_x = vertex_x - mean_px
    delta_y = vertex_y - mean_py
    shift_x = mean_qx + lin_xx * delta_x + lin_xy * delta_y - vertex_x
    shift_y = mean_qy + lin_yx * delta_x + lin_yy * delta_y - vertex_y
    return [lin_xx, lin_xy, lin_yx, lin_yy, shift_x, shift_y]


GROUPS = H // SP
FIRST = 8
UB = 16
UP = 4
MORE = 2
PER = 7


def pick(x, lanes):
    dims = lax.GatherDimensionNumbers(
        offset_dims=(), collapsed_slice_dims=(1,), start_index_map=(1,),
        operand_batching_dims=(0,), start_indices_batching_dims=(0,))
    return lax.gather(x, lanes[..., None], dims, slice_sizes=(1, 1),
                      mode=lax.GatherScatterMode.PROMISE_IN_BOUNDS)


def page_rows(rows_ref, to, there):
    lanes = lax.broadcasted_iota(jnp.int32, (H, 128), 1)
    zero = jnp.zeros((H, 128), jnp.bfloat16)
    prev = [zero, zero]
    for k in range(W // 128 + 1):
        now = zero
        if k < W // 128:
            now = rows_ref[:, 128 * k : 128 * k + 128]
            if there is not None:
                now = jnp.where(there, now, zero)
        for p, turn in enumerate((64, 63)):
            turned = pltpu.roll(now, turn, 1) if k < W // 128 else zero
            to[p, :, 128 * k : 128 * k + 128] = jnp.where(lanes < turn, prev[p], turned)
            prev[p] = turned


def positions(shifts, ext, num_ref, sp_s, low_s, far_s, ix_s, w0_s, w1_s):
    blocks = W // 128
    f32 = jnp.float32
    left, right = shifts[:, 0:128], shifts[:, 128:256]
    lane16 = lax.broadcasted_iota(jnp.int32, (16, 128), 1)
    ext[0] = jnp.where(lane16 < 1, left[:, 0:1], pltpu.roll(left, 1, 1))
    ext[1] = jnp.where(lane16 < 17, pltpu.roll(left, 17, 1), pltpu.roll(right, 17, 1))
    ext[2] = jnp.where(lane16 < 33, pltpu.roll(right, 33, 1), right[:, 127:128])

    sub = lax.broadcasted_iota(jnp.int32, (8, 128), 0)
    subf = sub.astype(f32)
    lane = lax.broadcasted_iota(jnp.int32, (8, 128), 1)
    wa = jnp.maximum(0.0, 1.0 - (subf + 4.0) * (1.0 / SP))
    wb = jnp.maximum(0.0, 1.0 - jnp.abs(subf - 4.0) * (1.0 / SP))
    wc = jnp.maximum(0.0, 1.0 - (12.0 - subf) * (1.0 / SP))
    wa, wb, wc = H * wa, H * wb, H * wc
    column = lane.astype(f32) + 64.0
    step = (lane + SP // 2) // SP
    part = ((lane + SP // 2) % SP).astype(f32) * (1.0 / SP)

    def prepare(b, spans):
        page = b // PER
        at = step + (b - page * PER) * (128 // SP)
        fine = []
        for half in range(2):
            held = ext[page, 8 * half : 8 * half + 8, :]
            near = pick(held, at)
            fine.append(near + part * (pick(held, at + 1) - near))
        fx, fy = fine
        most = None
        for g in range(GROUPS):
            dx = wa * fx[g : g + 1] + wb * fx[g + 1 : g + 2] + wc * fx[g + 2 : g + 3]
            dy = wa * fy[g : g + 1] + wb * fy[g + 1 : g + 2] + wc * fy[g + 2 : g + 3]
            sy = jnp.clip((subf + 8.0 * g) + dy, -33.0, 64.0)
            lx = jnp.clip(column + dx, -1.0, 256.0)
            base = jnp.clip(jnp.floor(lx), 0.0, 255.0)
            past = lx - base
            taps = [1.0 - jnp.abs(past), jnp.maximum(jnp.minimum(past, 255.0 - base), 0.0)]
            low = jnp.floor(jnp.min(sy, axis=1, keepdims=True))
            rel = sy - low
            most = rel if most is None else jnp.maximum(most, rel)
            r, tall = slice(8 * g, 8 * g + 8), slice(16 * g, 16 * g + 16)
            sp_s[b, r, :] = rel
            low_s[b, r, :] = jnp.broadcast_to(low, (8, 128))
            far_s[b, r, :] = base
            at = base.astype(jnp.int32)
            ix_s[b, tall, :] = jnp.concatenate([at, at], axis=0).astype(jnp.int16)
            taps = jnp.concatenate(taps, axis=0).astype(jnp.bfloat16).astype(f32)
            w0_s[b, r, :] = taps[0:8]
            w1_s[b, r, :] = taps[8:16]
        return jnp.where(lane == b, jnp.max(most, axis=1, keepdims=True), spans)

    spans = jnp.zeros((8, 128), f32)
    for b in range(blocks):
        spans = prepare(b, spans)
    rows = jnp.floor(jnp.max(spans, axis=0, keepdims=True)).astype(jnp.int32) + 2
    extra = (jnp.maximum(rows - FIRST, 0) + (MORE - 1)) // MORE
    extra = jnp.where(lane[0:1] == blocks, jnp.max(extra, axis=1, keepdims=True), extra)
    num_ref[...] = jnp.broadcast_to(extra, (8, 128))


OFFSETS = (1, -1, 2, -2)
FAR = 1e5
RATE = -2.0 * math.log2(math.e)
SKIP = 1e3


def halves(x):
    high = x.astype(jnp.bfloat16)
    return high, (x - high.astype(jnp.float32)).astype(jnp.bfloat16)


def fit_kernel(pts_ref, src_ref, fit_ref, num_ref, sp_s, low_s, far_s, ix_s, w0_s, w1_s, paged, wide,
               rows_s, ext, held, staged, mom, side, send_p, recv_p, send_s, recv_s, load):
    f32 = jnp.float32
    me = lax.axis_index("ty")
    n = lax.axis_size("ty")
    half = pts_ref.shape[1] // 2
    pairs = W // 256

    def exists(d):
        return (me + d >= 0) & (me + d < n)

    own_points = [
        pltpu.make_async_copy(pts_ref.at[:, pl.ds(c * half, half)], held.at[2, pl.ds(4 * c, 4)], load.at[c])
        for c in range(2)
    ]
    for c in own_points:
        c.start()
    own_rows = pltpu.make_async_copy(src_ref, rows_s, load.at[2])
    own_rows.start()
    barrier = pltpu.get_barrier_semaphore()
    for d in OFFSETS:
        @pl.when(exists(d))
        def _(d=d):
            pl.semaphore_signal(barrier, inc=1, device_id={"ty": me + d}, device_id_type=MESH)
    peers = sum(exists(d).astype(jnp.int32) for d in OFFSETS)

    def points_to(i, d):
        return pltpu.make_async_remote_copy(
            src_ref=held.at[2], dst_ref=held.at[2 - d], send_sem=send_p.at[i], recv_sem=recv_p.at[i],
            device_id={"ty": me + d}, device_id_type=MESH)

    def source_to(i, d):
        return pltpu.make_async_remote_copy(
            src_ref=src_ref, dst_ref=wide.at[i], send_sem=send_s.at[i], recv_sem=recv_s.at[i],
            device_id={"ty": me + d}, device_id_type=MESH)

    for c in own_points:
        c.wait()
    pl.semaphore_wait(barrier, peers)
    for i, d in enumerate(OFFSETS):
        @pl.when(exists(d))
        def _(i=i, d=d):
            points_to(i, d).start()
    for i, d in enumerate(OFFSETS[:2]):
        @pl.when(exists(d))
        def _(i=i, d=d):
            source_to(i, d).start()

    wide_lane = lax.broadcasted_iota(jnp.int32, (8, half + 128), 1) // 128
    wide_row = lax.broadcasted_iota(jnp.int32, (8, half + 128), 0) % 2
    centre = (me * H).astype(f32) + H / 2.0
    anchors = [
        jnp.where(wide_row == 0, ((2 * wide_lane + odd) * 256 + 128).astype(f32), centre) * (1.0 / H)
        for odd in range(2)
    ]
    spare = jnp.full((8, 128), FAR, f32)

    def stage(tile):
        data = held[2] if tile == 2 else jnp.where(exists(tile - 2), held[tile], FAR)
        row = jnp.concatenate([data, spare], axis=1) * (1.0 / H)
        staged[0, tile] = pltpu.roll(row, 32, 1) - anchors[0]
        staged[1, tile] = pltpu.roll(row, half + 96, 1) - anchors[1]

    e = lax.broadcasted_iota(jnp.int32, (8, 128), 0)
    vy = (((e - 1) * SP + SP // 2) - H // 2).astype(f32) * (1.0 / H)
    vy_of = {1: jnp.where(e == 5, SKIP, vy), 2: vy, 3: jnp.where(e == 0, SKIP, vy)}
    lone = {0: (-SP // 2 - H // 2) / H, 4: (4 * SP + SP // 2 - H // 2) / H}
    lane32 = lax.broadcasted_iota(jnp.int32, (32, 128), 1)
    vert32 = lax.broadcasted_iota(jnp.int32, (32, 128), 0)
    near = jnp.abs(lane32 // 32 - 1 - vert32 // 16) <= 1
    vx = jnp.where(near, (vert32 * SP + SP // 2 - 128).astype(f32) * (1.0 / H), SKIP)

    def bell(gap):
        return jnp.exp2((gap * gap) * RATE)

    def rows_of(k, odd, tile, c):
        at = pl.ds(pl.multiple_of(k * 128, 128), 128)
        return [jnp.broadcast_to(staged[odd, tile, 4 * c + i : 4 * c + i + 1, at], (8, 128)) for i in range(4)]

    def across(px):
        gap = jnp.concatenate([px - vx[8 * g : 8 * g + 8] for g in range(4)], axis=0)
        return jnp.concatenate(halves(bell(gap)), axis=0)

    def contract(parts, weights):
        return lax.dot_general(
            jnp.concatenate(parts, axis=1), jnp.concatenate(weights, axis=1),
            (((1,), (1,)), ((), ())), preferred_element_type=f32)

    def dense(k, odd, tiles):
        parts, weights = [], []
        for tile in tiles:
            for c in range(2):
                px, py, qx, qy = rows_of(k, odd, tile, c)
                weights.append(across(px))
                w = bell(py - vy_of[tile])
                wpx = w * px
                wpy = w * py
                feats = jnp.concatenate(
                    [w, wpx, wpy, w * qx, w * qy, wpx * px, wpx * py, wpy * py,
                     wpx * qx, wpy * qx, wpx * qy, wpy * qy], axis=0)
                parts.append(jnp.concatenate(halves(feats), axis=0))
        got = contract(parts, weights)
        got = got[0:96] + got[96:192]
        return got[:, 0:32] + got[:, 32:64]

    def single(k, odd, tile):
        parts, weights = [], []
        for c in range(2):
            px, py, qx, qy = rows_of(k, odd, tile, c)
            weights.append(across(px))
            w = bell(py - lone[tile])
            a1 = jnp.where(e == 0, 1.0, jnp.where((e == 2) | (e == 7), py, jnp.where(e == 3, qx, jnp.where(e == 4, qy, px))))
            b1 = jnp.where(e < 5, 1.0, jnp.where(e == 5, px, py))
            a2 = jnp.where(e % 2 == 0, px, py)
            b2 = jnp.where(e < 2, qx, qy)
            feats = jnp.concatenate([w * a1 * b1, w * a2 * b2], axis=0)
            parts.append(jnp.concatenate(halves(feats), axis=0))
        got = contract(parts, weights)
        got = got[0:16] + got[16:32]
        return got[:, 0:32] + got[:, 32:64]

    def own_group(k, _):
        for odd in range(2):
            mom[2 * k + odd] = dense(k, odd, (2,))
        return 0

    def next_group(k, _):
        for odd in range(2):
            mom[2 * k + odd] += dense(k, odd, (1, 3))
        return 0

    def last_group(k, _):
        for odd in range(2):
            for s, tile in enumerate((0, 4)):
                side[s, 2 * k + odd] = single(k, odd, tile)
        return 0

    def arrive(which):
        for i in which:
            @pl.when(exists(-OFFSETS[i]))
            def _(i=i):
                points_to(i, OFFSETS[i]).wait_recv()
        for i in which:
            stage(2 - OFFSETS[i])

    stage(2)
    lax.fori_loop(0, pairs // 2, own_group, 0, unroll=4)
    own_rows.wait()
    page_rows(rows_s, paged, None)
    arrive((0, 1))
    lax.fori_loop(0, pairs // 2, next_group, 0, unroll=4)
    arrive((2, 3))
    lax.fori_loop(0, pairs // 2, last_group, 0, unroll=4)

    ew = lax.broadcasted_iota(jnp.int32, (8, VC), 0)
    jw = lax.broadcasted_iota(jnp.int32, (8, VC), 1)
    vertex_y = (((ew - 1) * SP + SP // 2) - H // 2).astype(f32) * (1.0 / H)
    vertex_x = ((jw % 32) * SP + SP // 2 - 128).astype(f32) * (1.0 / H)
    safe = ew < 6
    sides = [jnp.concatenate([side[s, g] for g in range(pairs)], axis=1) for s in range(2)]
    moments = []
    for f in range(12):
        m = jnp.concatenate([mom[g, 8 * f : 8 * f + 8, :] for g in range(pairs)], axis=1)
        m = m + jnp.where(ew == 0, sides[0][f : f + 1], jnp.where(ew == 5, sides[1][f : f + 1], 0.0))
        moments.append(m)
    moments[0] = jnp.where(safe, moments[0], 1.0)
    solved = solve_affine(moments, vertex_x, vertex_y)
    for f in range(6):
        x = solved[f]
        if f >= 4:
            x = jnp.where((ew == 0) & (me == 0), x[1:2], x)
            x = jnp.where((ew == 5) & (me == n - 1), x[4:5], x)
            x = jnp.where(safe, x, 0.0)
        fit_ref[8 * f : 8 * f + 8, :] = x
        solved[f] = x
    positions(jnp.concatenate(solved[4:6], axis=0), ext, num_ref, sp_s, low_s, far_s, ix_s, w0_s, w1_s)

    for i, d in enumerate(OFFSETS[:2]):
        @pl.when(exists(-d))
        def _(i=i, d=d):
            source_to(i, d).wait_recv()
    for i, d in enumerate(OFFSETS):
        @pl.when(exists(d))
        def _(i=i, d=d):
            points_to(i, d).wait_send()
    for i, d in enumerate(OFFSETS[:2]):
        @pl.when(exists(d))
        def _(i=i, d=d):
            source_to(i, d).wait_send()


def fit(points, source):
    size = points.shape[1]
    blocks = W // 128
    per = lambda d: pltpu.VMEM((blocks, H, 128), d)
    vm = pl.BlockSpec(memory_space=pltpu.VMEM)
    return pl.pallas_call(
        fit_kernel,
        out_shape=(
            pltpu.VMEM((48, VC), jnp.float32),
            pltpu.VMEM((8, 128), jnp.int32),
            per(jnp.float32), per(jnp.float32), per(jnp.float32),
            pltpu.VMEM((blocks, 2 * H, 128), jnp.int16),
            per(jnp.float32), per(jnp.float32),
            pltpu.VMEM((2, H, W + 128), jnp.bfloat16),
            pltpu.VMEM((2, H, W), jnp.bfloat16),
        ),
        in_specs=[pl.BlockSpec(memory_space=pltpu.HBM)] * 2,
        out_specs=(vm,) * 10,
        scratch_shapes=[
            pltpu.VMEM((H, W), jnp.bfloat16),
            pltpu.VMEM((-(-blocks // PER), 16, 128), jnp.float32),
            pltpu.VMEM((5, 8, size // 2), jnp.float32),
            pltpu.VMEM((2, 5, 8, size // 2 + 128), jnp.float32),
            pltpu.VMEM((W // 256, 96, 32), jnp.float32),
            pltpu.VMEM((2, W // 256, 16, 32), jnp.float32),
            pltpu.SemaphoreType.DMA((4,)),
            pltpu.SemaphoreType.DMA((4,)),
            pltpu.SemaphoreType.DMA((2,)),
            pltpu.SemaphoreType.DMA((2,)),
            pltpu.SemaphoreType.DMA((3,)),
        ],
        compiler_params=pltpu.CompilerParams(collective_id=0, has_side_effects=True, vmem_limit_bytes=8 << 20),
        name="fit",
    )(points, source)


def render_kernel(first_ref, count_ref, fit_ref, num_ref, sp_s, low_s, far_s, ix_s, w0_s, w1_s, paged, wide_ref,
                  out_ref, aff_ref, halo, accum, num_m, sem):
    blocks = W // 128
    tile = lax.axis_index("ty")
    n = lax.axis_size("ty")
    f32 = jnp.float32
    bring = pltpu.make_async_copy(num_ref, num_m, sem)
    bring.start()
    for f in range(6):
        aff_ref[f] = fit_ref[8 * f + 1 : 8 * f + 5, :]

    page_rows(wide_ref.at[0], halo.at[0], tile > 0)
    page_rows(wide_ref.at[1], halo.at[1], tile < n - 1)
    slot = lax.broadcasted_iota(jnp.int32, (8, 3 * H), 1)
    first = jnp.broadcast_to(first_ref[...].reshape(1, 1), slot.shape) * BH - tile * H + H
    last = first + jnp.broadcast_to(count_ref[...].reshape(1, 1), slot.shape) * BH
    slot = jnp.where((slot >= first) & (slot < last), (slot - H).astype(f32), -1e6)

    def source_of(b):
        cols = pl.ds(pl.multiple_of(b * 128, 128), 256)
        window = [
            jnp.concatenate([halo[0, p, :, cols], paged[p, :, cols], halo[1, p, :, cols]], axis=0) for p in range(2)]
        lows = [low_s[b, 8 * g : 8 * g + 8, :][:, : 3 * H] for g in range(GROUPS)]
        return window, lows

    def pull(held, start, size):
        window, lows = held
        onehot = jnp.concatenate(
            [jnp.where(slot == lows[g] + (start + d), 1.0, 0.0) for g in range(GROUPS) for d in range(size)], axis=0)
        onehot = onehot.astype(jnp.bfloat16)
        return [jnp.dot(onehot, w, preferred_element_type=f32) for w in window]

    def blend(b, got, start, size, accs):
        out = []
        for g in range(GROUPS):
            r = slice(8 * g, 8 * g + 8)
            lanes_at = ix_s[b, 16 * g : 16 * g + 16, :]
            m = lanes_at & 127
            here = far_s[b, r, :] < 128.0
            rel = sp_s[b, r, :]
            totals = [None, None]
            for d in range(size):
                at = slice(8 * (g * size + d), 8 * (g * size + d) + 8)
                near, far = [
                    jnp.concatenate([tap[at, side] for tap in got], axis=0).astype(jnp.bfloat16)
                    for side in (slice(0, 128), slice(128, 256))
                ]
                near, far = pick(near, m).astype(f32), pick(far, m).astype(f32)
                ty = jnp.maximum(0.0, 1.0 - jnp.abs(rel - (start + d)))
                for p in range(2):
                    term = jnp.where(here, near[8 * p : 8 * p + 8], far[8 * p : 8 * p + 8]) * ty
                    totals[p] = term if d == 0 else totals[p] + term
            res = totals[0] * w0_s[b, r, :] + totals[1] * w1_s[b, r, :]
            out.append(res if accs[g] is None else accs[g] + res)
        return tuple(out)

    def paint(q, _):
        bs = [q * UB + j for j in range(UB)]
        gots = [pull(source_of(b), 0.0, FIRST) for b in bs]
        for b, got in zip(bs, gots):
            accum[b] = jnp.concatenate(blend(b, got, 0.0, FIRST, (None,) * GROUPS), axis=0)
        return 0

    lax.fori_loop(0, blocks // UB, paint, 0)
    bring.wait()

    @pl.when(num_m[0, blocks] > 0)
    def _():
        def again(b, _):
            def more(k, accs):
                start = (FIRST + MORE * k).astype(f32)
                return blend(b, pull(source_of(b), start, MORE), start, MORE, accs)

            @pl.when(num_m[0, b] > 0)
            def _():
                accs = tuple(accum[b, 8 * g : 8 * g + 8, :] for g in range(GROUPS))
                accum[b] = jnp.concatenate(lax.fori_loop(0, num_m[0, b], more, accs), axis=0)

            return 0

        lax.fori_loop(0, blocks, again, 0)

    def emit(b, _):
        out_ref[:, pl.ds(pl.multiple_of(b * 128, 128), 128)] = accum[b].astype(jnp.bfloat16)
        return 0
    lax.fori_loop(0, blocks, emit, 0, unroll=4)


def render(first, count, fitted):
    vm = pl.BlockSpec(memory_space=pltpu.VMEM)
    return pl.pallas_call(
        render_kernel,
        out_shape=(
            jax.ShapeDtypeStruct((H, W), jnp.bfloat16),
            jax.ShapeDtypeStruct((6, VR, VC), jnp.float32),
        ),
        in_specs=[vm] * (2 + len(fitted)),
        out_specs=(vm, vm),
        scratch_shapes=[
            pltpu.VMEM((2, 2, H, W + 128), jnp.bfloat16),
            pltpu.VMEM((W // 128, H, 128), jnp.float32),
            pltpu.SMEM((8, 128), jnp.int32),
            pltpu.SemaphoreType.DMA,
        ],
        compiler_params=pltpu.CompilerParams(vmem_limit_bytes=16 << 20),
        name="render",
    )(first, count, *fitted)


def per_device(points, source, slab_first, slab_count):
    points, source = [pltpu.with_memory_space_constraint(x, pltpu.HBM) for x in (points, source)]
    return render(slab_first, slab_count, fit(points, source))


def solution(mesh):
    return jax.shard_map(
        per_device,
        mesh=mesh,
        in_specs=(
            P(None, ("sec", "ty")),
            P(("sec", "ty"), None),
            P(("sec", "ty")),
            P(("sec", "ty")),
        ),
        out_specs=(P(("sec", "ty"), None), P(None, ("sec", "ty"), None)),
        check_vma=False,
    )
```

profile of v0, /device:TPU:9, one launch (start us, length us, event | category | flops | bytes accessed | tf_op | source)
XLA Modules:
  0.0 13.0 jit_solution(6106096211512959506)
XLA Ops:
  1.9 8.4 %fit.1 = (f32[48,256]{1,0:T(8,128)S(1)}, s32[8,128]{1,0:T(8,128)S(1)}, f32[16,32,128]{2,1,0:T(8,128)S(1)}, f32[16,32,128]{2,1,0:T(8,128)S(1)}, f32[16,32,128]{2,...) custom-call(f32[4,1024]{1,0:T(4,128)} %pts_ref.1, ...), custom_call_target="tpu_custom_call" | custom-call | tf_op jit(solution)/shard_map/fit/pallas_call | solution.py:345
  10.4 2.6 %render.1 = (bf16[32,2048]{1,0:T(8,128)(2,1)}, f32[6,4,256]{2,1,0:T(4,128)}) custom-call(s32[1]{0:T(128)S(6)} %copy.6.first_ref, s32[1]{0:T(128)S(6)} %copy.7.count_ref, f32[48,256]{1,0:T(8,128)S(1)} %get-tuple-element.12.fit_ref, s32[8,128]{1,0:T(8,128)S(1)} %get-tuple-element.13.num_ref, f32[16,32,128]{2,1,0:T(8,128)S(1)} %get-tuple-element.14.sp_s, ...), custom_call_target="tpu_custom_call" | custom-call | tf_op jit(solution)/shard_map/render/pallas_call | solution.py:466
where the time goes:
time: 13.2 us; the launch traced here: 13 us
  Pallas kernels  11 us (83%)
  between operations  1.93 us (15%)
    pallas_call x1, Pallas kernels, fit(): pl.pallas_call(fit_kernel, out_shape=(pltpu.VMEM((48, VC), jnp.float32),...  8.44 us
    pallas_call x1, Pallas kernels, render(): pl.pallas_call(render_kernel, out_shape=(jax.ShapeDtypeStruct((H, W), jnp...  2.59 us

commit v1 on v0

--- a/solution.py
+++ b/solution.py
@@ -43,7 +43,7 @@
 
 
 GROUPS = H // SP
-FIRST = 8
+FIRST = 9
 UB = 16
 UP = 4
 MORE = 2
@@ -395,13 +395,13 @@
         cols = pl.ds(pl.multiple_of(b * 128, 128), 256)
         window = [
             jnp.concatenate([halo[0, p, :, cols], paged[p, :, cols], halo[1, p, :, cols]], axis=0) for p in range(2)]
-        lows = [low_s[b, 8 * g : 8 * g + 8, :][:, : 3 * H] for g in range(GROUPS)]
+        lows = [slot - low_s[b, 8 * g : 8 * g + 8, :][:, : 3 * H] for g in range(GROUPS)]
         return window, lows
 
     def pull(held, start, size):
         window, lows = held
         onehot = jnp.concatenate(
-            [jnp.where(slot == lows[g] + (start + d), 1.0, 0.0) for g in range(GROUPS) for d in range(size)], axis=0)
+            [jnp.where(lows[g] == start + d, 1.0, 0.0) for g in range(GROUPS) for d in range(size)], axis=0)
         onehot = onehot.astype(jnp.bfloat16)
         return [jnp.dot(onehot, w, preferred_element_type=f32) for w in window]
 
@@ -414,6 +414,7 @@
             here = far_s[b, r, :] < 128.0
             rel = sp_s[b, r, :]
             totals = [None, None]
+            last = jnp.clip(rel - (start - 1.0), 0.0, 1.0)
             for d in range(size):
                 at = slice(8 * (g * size + d), 8 * (g * size + d) + 8)
                 near, far = [
@@ -421,7 +422,9 @@
                     for side in (slice(0, 128), slice(128, 256))
                 ]
                 near, far = pick(near, m).astype(f32), pick(far, m).astype(f32)
-                ty = jnp.maximum(0.0, 1.0 - jnp.abs(rel - (start + d)))
+                ramp = jnp.clip(rel - (start + d), 0.0, 1.0)
+                ty = last - ramp
+                last = ramp
                 for p in range(2):
                     term = jnp.where(here, near[8 * p : 8 * p + 8], far[8 * p : 8 * p + 8]) * ty
                     totals[p] = term if d == 0 else totals[p] + term
@@ -429,11 +432,16 @@
             out.append(res if accs[g] is None else accs[g] + res)
         return tuple(out)
 
+    def put(b, rows):
+        rows = jnp.concatenate(rows, axis=0)
+        accum[b] = rows
+        out_ref[:, pl.ds(b * 128 if isinstance(b, int) else pl.multiple_of(b * 128, 128), 128)] = rows.astype(jnp.bfloat16)
+
     def paint(q, _):
         bs = [q * UB + j for j in range(UB)]
         gots = [pull(source_of(b), 0.0, FIRST) for b in bs]
         for b, got in zip(bs, gots):
-            accum[b] = jnp.concatenate(blend(b, got, 0.0, FIRST, (None,) * GROUPS), axis=0)
+            put(b, blend(b, got, 0.0, FIRST, (None,) * GROUPS))
         return 0
 
     lax.fori_loop(0, blocks // UB, paint, 0)
@@ -449,16 +457,11 @@
             @pl.when(num_m[0, b] > 0)
             def _():
                 accs = tuple(accum[b, 8 * g : 8 * g + 8, :] for g in range(GROUPS))
-                accum[b] = jnp.concatenate(lax.fori_loop(0, num_m[0, b], more, accs), axis=0)
+                put(b, lax.fori_loop(0, num_m[0, b], more, accs))
 
             return 0
 
         lax.fori_loop(0, blocks, again, 0)
-
-    def emit(b, _):
-        out_ref[:, pl.ds(pl.multiple_of(b * 128, 128), 128)] = accum[b].astype(jnp.bfloat16)
-        return 0
-    lax.fori_loop(0, blocks, emit, 0, unroll=4)
 
 
 def render(first, count, fitted):

time: 13.2 us -> 13.5 us (1.023); the launches traced: 13 us -> 13.5 us
  Pallas kernels: 11 us -> 11.5 us
    pallas_call x1, Pallas kernels: 2.59 us -> 3.1 us  [render(): pl.pallas_call(render_kernel, out_shape=(jax.ShapeDtypeStruct((H, W), jnp...]
where the time goes in v1:
time: 13.5 us
  Pallas kernels  11.5 us (85%)
  between operations  1.93 us (14%)
    pallas_call x1, Pallas kernels, fit(): pl.pallas_call(fit_kernel, out_shape=(pltpu.VMEM((48, VC), jnp.float32),...  8.44 us
    pallas_call x1, Pallas kernels, render(): pl.pallas_call(render_kernel, out_shape=(jax.ShapeDtypeStruct((H, W), jnp...  3.1 us

profile of v1, /device:TPU:9, one launch (start us, length us, event | category | flops | bytes accessed | tf_op | source)
XLA Modules:
  0.0 13.5 jit_solution(13062334277740037530)
XLA Ops:
  1.9 8.4 %fit.1 = (f32[48,256]{1,0:T(8,128)S(1)}, s32[8,128]{1,0:T(8,128)S(1)}, f32[16,32,128]{2,1,0:T(8,128)S(1)}, f32[16,32,128]{2,1,0:T(8,128)S(1)}, f32[16,32,128]{2,...) custom-call(f32[4,1024]{1,0:T(4,128)} %pts_ref.1, ...), custom_call_target="tpu_custom_call" | custom-call | tf_op jit(solution)/shard_map/fit/pallas_call | solution.py:345
  10.4 3.1 %render.1 = (bf16[32,2048]{1,0:T(8,128)(2,1)}, f32[6,4,256]{2,1,0:T(4,128)}) custom-call(s32[1]{0:T(128)S(6)} %copy.6.first_ref, s32[1]{0:T(128)S(6)} %copy.7.count_ref, f32[48,256]{1,0:T(8,128)S(1)} %get-tuple-element.12.fit_ref, s32[8,128]{1,0:T(8,128)S(1)} %get-tuple-element.13.num_ref, f32[16,32,128]{2,1,0:T(8,128)S(1)} %get-tuple-element.14.sp_s, ...), custom_call_target="tpu_custom_call" | custom-call | tf_op jit(solution)/shard_map/render/pallas_call | solution.py:469
